TPU v7x, 32 devices: a whole 2x2x4 slice. The times are simulated.
32 devices in a mesh: dp: 8 (over z, x), tp: 4 (over y, core).
Axes of the slice: x: 2, y: 2, z: 4, core: 2. Of those that a mesh axis runs over, the one named last changes fastest.
Arguments:
- slopes: bfloat16 [8, 2, 3072, 768], P('dp', None, 'tp'), may hold values from -6 to 6, as said below
- basis_in: float32 [2, 768, 8], replicated, may hold values from -6 to 6
- weights_in: float32 [2, 3072, 768], P(None, 'tp', 'dp'), may hold values from -0.21875 to 0.21875
Outputs:
- new_weights: float32 [2, 3072, 768], P(None, 'tp', 'dp')
- new_basis: float32 [2, 768, 8], replicated
Inputs may be any that keep to these rules, and one draw needn't show every extreme that they name: slopes holds numbers from -6 to 6.
All inputs are finite; a program needn't handle non-finite values.
Results may differ from a plain program's by a relative error of at most 0.0003.
Values sent between devices are 32-bit elements.
A program may use at most 64 MiB of HBM per device.

v0:
```python
import jax
import jax.numpy as jnp
from jax import lax
from jax.sharding import PartitionSpec as P

RANK = 8


def body(slopes, basis_in, weights_in):
    own_grads = slopes[0]
    part_left = jnp.einsum(
        "liw,lwr->lir", own_grads, basis_in.astype(jnp.bfloat16), preferred_element_type=jnp.float32
    )
    left = lax.psum(part_left, "dp")
    part_gram = jnp.einsum("lir,lis->lrs", left, left, precision=lax.Precision.HIGHEST)
    small_left = left.astype(jnp.bfloat16)
    part_right = jnp.einsum(
        "liw,lir->lwr", own_grads, small_left, preferred_element_type=jnp.float32
    )
    own_share = part_gram / lax.axis_size("dp")
    right, gram = lax.psum((part_right, own_share), ("dp", "tp"))
    gram = gram + 0.001 * jnp.mean(jnp.diagonal(gram, axis1=1, axis2=2), axis=1)[
        :, None, None
    ] * jnp.eye(RANK, dtype=jnp.float32)
    place = lax.axis_index("dp") * weights_in.shape[2]
    own_right = lax.dynamic_slice_in_dim(right, place, weights_in.shape[2], axis=1)
    root = jnp.linalg.cholesky(gram)
    half = lax.linalg.triangular_solve(
        root, jnp.swapaxes(own_right, 1, 2), left_side=True, lower=True
    )
    mixed = lax.linalg.triangular_solve(root, half, left_side=True, lower=True, transpose_a=True)
    change = jnp.einsum(
        "lir,lrw->liw", left, mixed, precision=lax.Precision.HIGHEST
    ) / lax.axis_size("dp")
    new_weights = weights_in - 0.02 * change
    new_basis = right * lax.rsqrt(jnp.mean(right * right, axis=(1, 2), keepdims=True) + 1e-12)
    return (new_weights, new_basis)


def solution(mesh):
    placed = (P("dp", None, "tp", None), P(), P(None, "tp", "dp"))
    return jax.shard_map(
        body, mesh=mesh, in_specs=placed, out_specs=(P(None, "tp", "dp"), P()), check_vma=False
    )
```

profile of v0, /device:TPU:14, one launch (start us, length us, event | category | flops | bytes accessed | tf_op | source)
XLA Modules:
  0.0 88.3 jit_solution(12999612383202632761)
XLA Ops:
  0.6 0.0 copy-start
  0.7 0.1 copy.11
  0.8 1.5 %copy-done = bf16[1,2,768,768]{3,2,1,0:T(8,128)(2,1)S(1)} copy-done((bf16[1,2,768,768]{3,2,1,0:T(8,128)(2,1)S(1)}, bf16[1,2,768,768]{3,2,1,0:T(8,128)(2,1)}, u32[]{:S(2)}) %copy-start) | copy-done | bytes 2359320
  2.3 0.0 copy-start.1
  2.3 1.6 %fusion.2 = f32[2,768,8]{1,2,0:T(8,128)S(1)} fusion(bf16[1,2,768,768]{3,2,1,0:T(8,128)(2,1)S(1)} %copy-done, f32[2,768,8]{1,2,0:T(8,128)} %param.4), kind=kOutput, calls=%fused_computation.3 | convolution fusion | flops 18886656 | bytes 2457600 | tf_op jit(solution)/shard_map/liw,lwr->lir/dot_general | solution.py:11
  3.9 30.6 %psum.21 = f32[2,768,8]{1,2,0:T(8,128)S(1)} all-reduce(f32[2,768,8]{1,2,0:T(8,128)S(1)} %fusion.2), channel_id=1, replica_groups=mesh['dp'=8,'tp'=4] {'dp'}, use_global_device_ids=true, to_apply=%region_0.0 | all-reduce | flops 12288 | bytes 98304 | tf_op jit(solution)/shard_map/psum | solution.py:14
  34.4 0.2 convolution_multiply_fusion.1
  34.6 0.4 fusion.5
  35.0 46.7 %all-reduce = (f32[2,8,8]{1,2,0:T(8,128)S(1)}, f32[2,768,8]{1,2,0:T(8,128)S(1)}) all-reduce(f32[2,8,8]{1,2,0:T(8,128)S(1)} %convolution_multiply_fusion.1, f32[2,768,8]{1,2,0:T(8,128)S(1)} %fusion.5), channel_id=1, replica_groups=mesh['dp'=8,'tp'=4] {'dp','tp'}, use_global_device_ids=true, to_apply=%region_1.0 | all-reduce | flops 12416 | bytes 99328 | tf_op jit(solution)/shard_map/psum | solution.py:21
  81.7 0.1 multiply_reduce_fusion
  81.8 0.1 copy.13
  82.0 0.6 gather_fusion
  82.6 0.1 multiply_add_fusion
  82.6 0.1 copy.14
  82.7 0.1 fusion.14
  82.8 1.4 %custom-call.9 = f32[2,8,8]{2,1,0:T(8,128)S(1)} custom-call(f32[2,8,8]{2,1,0:T(8,128)S(1)} %fusion.14), custom_call_target="Cholesky" | custom-call | tf_op jit(solution)/shard_map/jit(cholesky)/cholesky | solution.py:27
  84.2 0.1 select_reduce_fusion
  84.3 0.1 compare_reduce_fusion
  84.4 0.1 select_bitcast_fusion
  84.5 1.3 %custom-call.10 = f32[2,1,8,8]{2,3,1,0:T(8,128)S(1)} custom-call(f32[2,1,8,8]{3,2,1,0:T(8,128)S(1)} %select_bitcast_fusion), custom_call_target="InvertDiagBlocksLowerTriangular" | custom-call | tf_op jit(solution)/shard_map/triangular_solve | solution.py:31
  85.7 0.2 fusion.10
  86.0 0.1 fusion.12
  86.1 0.7 broadcast_multiply_fusion
  86.8 0.0 copy-done.1
  86.8 1.5 %fusion.4 = f32[2,768,96]{1,2,0:T(8,128)} fusion(f32[2,768,96]{1,2,0:T(8,128)S(1)} %copy-done.1, f32[2,768,8]{1,2,0:T(8,128)S(1)} %psum.21, f32[2,8,96]{2,1,0:T(8,128)S(1)} %fusion.12), kind=kOutput, calls=%fused_computation.6 | convolution fusion | flops 14450688 | bytes 1234944 | tf_op jit(solution)/shard_map/lir,lrw->liw/dot_general | solution.py:32
  (7 shorter events, 0.1 us)
Async XLA Ops:
  0.6 1.7 %copy-start = (bf16[1,2,768,768]{3,2,1,0:T(8,128)(2,1)S(1)}, bf16[1,2,768,768]{3,2,1,0:T(8,128)(2,1)}, u32[]{:S(2)}) copy-start(bf16[1,2,768,768]{3,2,1,0:T(8,128)(2,1)} %param.3) | copy-start | bytes 7077892
  2.3 84.5 %copy-start.1 = (f32[2,768,96]{1,2,0:T(8,128)S(1)}, f32[2,768,96]{1,2,0:T(8,128)}, u32[]{:S(2)}) copy-start(f32[2,768,96]{1,2,0:T(8,128)} %param.5) | copy-start | bytes 1769476
where the time goes:
time: 88.6 us; the launch traced here: 88.3 us
  blocking collectives  77.2 us (87%)
  matrix products  4.02 us (5%)
  other arithmetic  3.96 us (4%)
  local copies, waits for them, and re-layouts  2.39 us (3%)
    psum x1, blocking collectives, body(): right, gram = lax.psum((part_right, own_share), ('dp', 'tp'))  46.7 us
    psum x1, blocking collectives, body(): left = lax.psum(part_left, 'dp')  30.6 us

commit v1 on v0

--- a/solution.py
+++ b/solution.py
@@ -6,12 +6,18 @@
 RANK = 8
 
 
+def summed_here(block, axis):
+    parts = lax.all_gather(block, axis, axis=0, tiled=False)
+    total = parts.sum(axis=0)
+    return total
+
+
 def body(slopes, basis_in, weights_in):
     own_grads = slopes[0]
     part_left = jnp.einsum(
         "liw,lwr->lir", own_grads, basis_in.astype(jnp.bfloat16), preferred_element_type=jnp.float32
     )
-    left = lax.psum(part_left, "dp")
+    left = summed_here(part_left, "dp")
     part_gram = jnp.einsum("lir,lis->lrs", left, left, precision=lax.Precision.HIGHEST)
     small_left = left.astype(jnp.bfloat16)
     part_right = jnp.einsum(

time: 88.6 us -> 84.4 us (0.953); the launches traced: 88.3 us -> 83 us
  blocking collectives: 77.2 us -> 71.9 us
    psum x1 -> x0, blocking collectives: 30.6 us -> none  [body(): left = lax.psum(part_left, 'dp')]
    all_gather x0 -> x1, blocking collectives: none -> 29.1 us  [summed_here(): parts = lax.all_gather(block, axis, axis=0, tiled=False)]
    psum x1, blocking collectives: 46.7 us -> 42.8 us  [body(): right, gram = lax.psum((part_right, own_share), ('dp', 'tp'))]
where the time goes in v1:
time: 84.4 us; the launch traced here: 83 us
  blocking collectives  71.9 us (85%)
  other arithmetic  3.99 us (5%)
  matrix products  3.96 us (5%)
  local copies, waits for them, and re-layouts  2.39 us (3%)
    psum x1, blocking collectives, body(): right, gram = lax.psum((part_right, own_share), ('dp', 'tp'))  42.8 us
    all_gather x1, blocking collectives, summed_here(): parts = lax.all_gather(block, axis, axis=0, tiled=False)  29.1 us

profile of v1, /device:TPU:14, one launch (start us, length us, event | category | flops | bytes accessed | tf_op | source)
XLA Modules:
  0.0 83.0 jit_solution(18143869499055249514)
XLA Ops:
  0.6 0.0 copy-start
  0.7 0.1 copy.17
  0.8 1.5 %copy-done = bf16[1,2,768,768]{3,2,1,0:T(8,128)(2,1)S(1)} copy-done((bf16[1,2,768,768]{3,2,1,0:T(8,128)(2,1)S(1)}, bf16[1,2,768,768]{3,2,1,0:T(8,128)(2,1)}, u32[]{:S(2)}) %copy-start) | copy-done | bytes 2359320
  2.3 1.5 %fusion.2 = f32[2,768,8]{1,2,0:T(8,128)S(1)} fusion(bf16[1,2,768,768]{3,2,1,0:T(8,128)(2,1)S(1)} %copy-done, f32[2,768,8]{1,2,0:T(8,128)} %param.4), kind=kOutput, calls=%fused_computation.3 | convolution fusion | flops 18886656 | bytes 2457600 | tf_op jit(solution)/shard_map/liw,lwr->lir/dot_general | solution.py:17
  3.8 0.0 copy-start.1
  3.8 29.1 %all-gather = f32[16,768,8]{1,2,0:T(8,128)S(1)} all-gather(f32[2,768,8]{1,2,0:T(8,128)S(1)} %fusion.2), channel_id=2, replica_groups=mesh['dp'=8,'tp'=4] {'dp'}, dimensions={0}, use_global_device_ids=true | all-gather | bytes 442368 | tf_op jit(solution)/shard_map/all_gather | solution.py:10
  32.9 0.2 convolution_multiply_fusion.1
  33.1 0.4 fusion.5
  33.6 42.8 %all-reduce = (f32[2,8,8]{1,2,0:T(8,128)S(1)}, f32[2,768,8]{1,2,0:T(8,128)S(1)}) all-reduce(f32[2,8,8]{1,2,0:T(8,128)S(1)} %convolution_multiply_fusion.1, f32[2,768,8]{1,2,0:T(8,128)S(1)} %fusion.5), channel_id=1, replica_groups=mesh['dp'=8,'tp'=4] {'dp','tp'}, use_global_device_ids=true, to_apply=%region_1.0 | all-reduce | flops 12416 | bytes 99328 | tf_op jit(solution)/shard_map/psum | solution.py:27
  76.4 0.1 multiply_reduce_fusion
  76.5 0.1 copy.19
  76.6 0.6 gather_fusion
  77.2 0.1 multiply_add_fusion
  77.3 0.1 copy.20
  77.4 0.1 fusion.14
  77.4 1.4 %custom-call.9 = f32[2,8,8]{2,1,0:T(8,128)S(1)} custom-call(f32[2,8,8]{2,1,0:T(8,128)S(1)} %fusion.14), custom_call_target="Cholesky" | custom-call | tf_op jit(solution)/shard_map/jit(cholesky)/cholesky | solution.py:33
  78.9 0.1 select_reduce_fusion
  78.9 0.1 compare_reduce_fusion
  79.1 0.1 select_bitcast_fusion
  79.1 1.3 %custom-call.10 = f32[2,1,8,8]{2,3,1,0:T(8,128)S(1)} custom-call(f32[2,1,8,8]{3,2,1,0:T(8,128)S(1)} %select_bitcast_fusion), custom_call_target="InvertDiagBlocksLowerTriangular" | custom-call | tf_op jit(solution)/shard_map/triangular_solve | solution.py:37
  80.4 0.2 fusion.10
  80.6 0.1 fusion.12
  80.8 0.7 broadcast_multiply_fusion
  81.5 0.0 copy-done.1
  81.5 1.5 %fusion.4 = f32[2,768,96]{1,2,0:T(8,128)} fusion(f32[2,768,96]{1,2,0:T(8,128)S(1)} %copy-done.1, f32[2,768,8]{1,2,0:T(8,128)S(1)} %reduce_sum.27, f32[2,8,96]{2,1,0:T(8,128)S(1)} %fusion.12), kind=kOutput, calls=%fused_computation.6 | convolution fusion | flops 14450688 | bytes 1234944 | tf_op jit(solution)/shard_map/lir,lrw->liw/dot_general | solution.py:38
  (8 shorter events, 0.1 us)
Async XLA Ops:
  0.6 1.7 %copy-start = (bf16[1,2,768,768]{3,2,1,0:T(8,128)(2,1)S(1)}, bf16[1,2,768,768]{3,2,1,0:T(8,128)(2,1)}, u32[]{:S(2)}) copy-start(bf16[1,2,768,768]{3,2,1,0:T(8,128)(2,1)} %param.3) | copy-start | bytes 7077892
  3.8 77.7 %copy-start.1 = (f32[2,768,96]{1,2,0:T(8,128)S(1)}, f32[2,768,96]{1,2,0:T(8,128)}, u32[]{:S(2)}) copy-start(f32[2,768,96]{1,2,0:T(8,128)} %param.5) | copy-start | bytes 1769476
